TPU v7x, 32 devices: a whole 2x2x4 slice. The times are simulated.
32 devices in a mesh: groups: 2 (over y), dp: 4 (over z), section: 2 (over x), tensor: 2 (over core).
Axes of the slice: x: 2, y: 2, z: 4, core: 2. Of those that a mesh axis runs over, the one named last changes fastest.
Arguments:
- hidden: bfloat16 [128, 8, 5120], P(('groups', 'dp')), parts along dimension 0, may hold values from -6 to 6
- unembed: bfloat16 [128, 8, 5120], P(('groups', 'dp')), parts along dimension 0, may hold values from -0.02734375 to 0.02734375
- value_proj: bfloat16 [2, 5120, 512], P('section', 'dp', 'tensor'), may hold values from -0.078125 to 0.078125
- output_proj: bfloat16 [2, 512, 5120], P('section', 'tensor', 'dp'), may hold values from -0.125 to 0.125
- norm_gains: float32 [2, 5120], P('section'), may hold values from 0.1 to 1.9
- survive: int32 [8], P(('groups', 'dp')), parts along dimension 0, may hold values from 0 to 1, as said below
- lengths: int32 [128], P(('groups', 'dp')), parts along dimension 0, may hold values from 1 to 8
- assign: int32 [128], P(('groups', 'dp')), parts along dimension 0, may hold values from 0 to 16, as said below
- advantage: float32 [128], P(('groups', 'dp')), parts along dimension 0, may hold values from -4 to 4
- reference_logit: float32 [128, 8], P(('groups', 'dp')), parts along dimension 0, may hold values from -4 to 4
- recorded_gap: float32 [128, 8], P(('groups', 'dp')), parts along dimension 0, may hold values from -2 to 2
Outputs:
- grad_value: float32 [4, 5120, 512], P(('groups', 'section'), 'dp', 'tensor'), parts along dimension 0
- grad_output: float32 [4, 512, 5120], P(('groups', 'section'), 'tensor', 'dp'), parts along dimension 0
There are 2 independent parts, one for each index of `groups`. A program takes and returns all parts, laid end to end along the dimension named above; an argument that names none is the same for every part. Nothing has to cross between parts.
Inputs may be any that keep to these rules, and one draw needn't show every extreme that they name: `survive`: 1 where the group of 16 responses is kept, 0 where it is dropped; in every draw all groups of some dp index are kept. `assign`: the 16 slots of a dp index list the local positions (0 to 15) of the responses of its kept groups, each exactly once, then hold 16 in every other slot.
All inputs are finite; a program needn't handle non-finite values.
Results may differ from a plain program's by a relative error of at most 0.029.
Values may be sent and summed in bfloat16 or wider, within the bound.
A program may use at most 64 MiB of HBM per device.

v0:
```python
import math
import jax
import jax.numpy as jnp
from jax import lax
from jax.sharding import PartitionSpec as P

GROUP = 16
MB_RESP = 8
eps_norm = 1e-06
loss_scale = 4096.0
clip_high = math.log(1.28)
clip_low = math.log(0.8)


def from_behind(block, axis, distance):
    devices = range(lax.axis_size(axis))
    route = [(i - distance, i) for i in devices if i - distance in devices]
    return lax.ppermute(block, axis, route)


def norm_forward(row_block, norm_gain):
    values = row_block.astype(jnp.float32)
    inverse = lax.rsqrt(jnp.mean(values * values, axis=-1, keepdims=True) + eps_norm)
    return (values, inverse, (values * inverse * norm_gain).astype(jnp.bfloat16))


def norm_backward(values, inverse, norm_gain, upstream):
    scaled = upstream * norm_gain
    inner_sum = jnp.sum(scaled * values, axis=-1, keepdims=True) / values.shape[-1]
    return inverse * scaled - values * (inverse * inverse * inverse) * inner_sum


def contract_last(left_rows, right_rows):
    return lax.dot_general(
        left_rows, right_rows, (((1,), (1,)), ((), ())), preferred_element_type=jnp.float32
    )


def contract_first(left_rows, right_rows):
    return lax.dot_general(
        left_rows, right_rows, (((0,), (0,)), ((), ())), preferred_element_type=jnp.float32
    )


def take_slot(slot_store, slot_index):
    return lax.dynamic_index_in_dim(slot_store, slot_index, 0, keepdims=False)


def put_slot(slot_store, new_value, slot_index, active):
    previous = take_slot(slot_store, slot_index)
    return lax.dynamic_update_index_in_dim(
        slot_store, jnp.where(active, new_value, previous), slot_index, 0
    )


def local(
    hidden,
    unembed,
    value_proj,
    output_proj,
    norm_gains,
    survive,
    lengths,
    assign,
    advantage,
    reference_logit,
    recorded_gap,
):
    resp_count = hidden.shape[0]
    positions = hidden.shape[1]
    model_width = hidden.shape[2]
    half_value = value_proj.shape[2]
    micro_count = resp_count // MB_RESP
    row_count = MB_RESP * positions
    section_count = lax.axis_size("section")
    section_index = lax.axis_index("section")
    is_last = section_index == section_count - 1
    norm_gain = norm_gains[0]
    alive_mask = jnp.repeat(survive, GROUP)
    local_count = jnp.sum((alive_mask * lengths).astype(jnp.float32))
    gathered_value, gathered_output = (
        lax.all_gather(value_proj, "dp", axis=1, tiled=True),
        lax.all_gather(output_proj, "dp", axis=2, tiled=True),
    )
    w_first = gathered_value[0]
    w_second = gathered_output[0]

    def pick(array):
        return jnp.take(array, assign, axis=0, mode="fill", fill_value=0)

    slot_hidden = pick(hidden).reshape(micro_count, row_count, model_width)
    slot_unembed = pick(unembed).reshape(micro_count, row_count, model_width)
    position_index = lax.broadcasted_iota(jnp.int32, (resp_count, positions), 1)
    live_mask = (position_index < pick(lengths)[:, None]).astype(jnp.float32)
    advantages = jnp.broadcast_to(pick(advantage)[:, None], (resp_count, positions))
    gap_rows = pick(recorded_gap)
    clipped = (advantages > 0) & (gap_rows > clip_high) | (advantages < 0) & (gap_rows < clip_low)
    kept_mask = 1.0 - clipped.astype(jnp.float32)
    weight_rows = (-loss_scale * advantages * kept_mask * live_mask).reshape(micro_count, row_count)
    logit_base = pick(reference_logit).reshape(micro_count, row_count)
    step_count = micro_count + section_count - 1
    store_in = jnp.zeros((micro_count, row_count, model_width), jnp.bfloat16)
    store_normed = jnp.zeros((micro_count, row_count, model_width), jnp.bfloat16)
    store_projected = jnp.zeros((micro_count, row_count, half_value), jnp.bfloat16)
    store_out = jnp.zeros((micro_count, row_count, model_width), jnp.bfloat16)
    arriving = jnp.zeros((row_count, model_width), jnp.bfloat16)
    for step_index in range(step_count):
        micro_index = step_index - section_index
        active = (micro_index >= 0) & (micro_index < micro_count)
        clamped = jnp.clip(micro_index, 0, micro_count - 1)
        entering = jnp.where(section_index == 0, take_slot(slot_hidden, clamped), arriving)
        values, inverse, normed = norm_forward(entering, norm_gain)
        projected = jnp.dot(normed, w_first, preferred_element_type=jnp.float32).astype(
            jnp.bfloat16
        )
        partial_out = jnp.dot(projected, w_second, preferred_element_type=jnp.float32)
        mixed_sum = lax.psum(partial_out.astype(jnp.bfloat16), "tensor").astype(jnp.float32)
        leaving = (values + mixed_sum).astype(jnp.bfloat16)
        store_in = put_slot(store_in, entering, clamped, active)
        store_normed = put_slot(store_normed, normed, clamped, active)
        store_projected = put_slot(store_projected, projected, clamped, active)
        store_out = put_slot(store_out, leaving, clamped, active)
        arriving = from_behind(leaving, "section", 1)
    store_upstream = jnp.zeros((micro_count, row_count, model_width), jnp.bfloat16)
    store_grad_value = jnp.zeros((micro_count, row_count, half_value), jnp.bfloat16)
    arriving = jnp.zeros((row_count, model_width), jnp.bfloat16)
    for step_index in range(step_count):
        micro_index = step_index - (section_count - 1 - section_index)
        active = (micro_index >= 0) & (micro_index < micro_count)
        clamped = jnp.clip(micro_index, 0, micro_count - 1)
        top_rows = take_slot(store_out, clamped).astype(jnp.float32)
        unembed_rows = take_slot(slot_unembed, clamped).astype(jnp.float32)
        logit = jnp.sum(top_rows * unembed_rows, axis=-1)
        seed_rows = take_slot(weight_rows, clamped) * jnp.exp(
            logit - take_slot(logit_base, clamped)
        )
        start_grad = (seed_rows[:, None] * unembed_rows).astype(jnp.bfloat16)
        upstream = jnp.where(is_last, start_grad, arriving)
        entering = take_slot(store_in, clamped)
        normed = take_slot(store_normed, clamped)
        projected = take_slot(store_projected, clamped)
        grad_projected = contract_last(upstream, w_second).astype(jnp.bfloat16)
        partial_norm = contract_last(grad_projected, w_first)
        grad_normed = lax.psum(partial_norm.astype(jnp.bfloat16), "tensor").astype(jnp.float32)
        values, inverse, unused_normed = norm_forward(entering, norm_gain)
        grad_entering = (
            upstream.astype(jnp.float32) + norm_backward(values, inverse, norm_gain, grad_normed)
        ).astype(jnp.bfloat16)
        store_upstream = put_slot(store_upstream, upstream, clamped, active)
        store_grad_value = put_slot(store_grad_value, grad_projected, clamped, active)
        arriving = from_behind(grad_entering, "section", -1)
    flat_normed = store_normed.reshape(micro_count * row_count, model_width)
    flat_upstream = store_upstream.reshape(micro_count * row_count, model_width)
    flat_grad_value = store_grad_value.reshape(micro_count * row_count, half_value)
    flat_projected = store_projected.reshape(micro_count * row_count, half_value)
    reduced = lax.psum_scatter(
        jnp.concatenate(
            [
                contract_first(flat_normed, flat_grad_value),
                contract_first(flat_upstream, flat_projected),
            ],
            axis=1,
        ).astype(jnp.bfloat16),
        "dp",
        scatter_dimension=0,
        tiled=True,
    ).astype(jnp.float32)
    token_total = lax.psum(local_count, "dp")
    scaled_grads = reduced / token_total
    grad_value = scaled_grads[:, :half_value][None]
    grad_output = scaled_grads[:, half_value:].T[None]
    return (grad_value, grad_output)


def solution(mesh):
    placed = (
        P(("groups", "dp"), None, None),
        P(("groups", "dp"), None, None),
        P("section", "dp", "tensor"),
        P("section", "tensor", "dp"),
        P("section", None),
        P(("groups", "dp")),
        P(("groups", "dp")),
        P(("groups", "dp")),
        P(("groups", "dp")),
        P(("groups", "dp"), None),
        P(("groups", "dp"), None),
    )
    return jax.shard_map(
        local,
        mesh=mesh,
        in_specs=placed,
        out_specs=(
            P(("groups", "section"), "dp", "tensor"),
            P(("groups", "section"), "tensor", "dp"),
        ),
        check_vma=False,
    )
```

profile of v0, /device:TPU:0, one launch (start us, length us, event | category | flops | bytes accessed | tf_op | source)
XLA Modules:
  0.0 449.3 jit_solution(629598408572374933)
XLA Ops:
  9.5 1.7 gather_fusion.2
  11.2 1.7 gather_fusion.4
  14.8 2.0 broadcast_select_fusion.1
  18.2 48.9 %all-gather.3.cloned.1.call-done = bf16[1,5120,256]{2,1,0:T(8,128)(2,1)} async-done(((bf16[1,1280,256]{2,1,0:T(8,128)(2,1)}), bf16[1,5120,256]{2,1,0:T(8,128)(2,1)}) %all-gather.3.cloned.1.call-update) | async-done | bytes 2621456 | tf_op jit(solution)/shard_map/all_gather | solution.py:82
  67.1 2.6 bitcast_dynamic-update-slice_fusion.10
  69.7 52.5 %all-gather.5.cloned.1.call-done = bf16[1,256,5120]{2,1,0:T(8,128)(2,1)} async-done(((bf16[1,256,1280]{2,1,0:T(8,128)(2,1)}), bf16[1,256,5120]{2,1,0:T(8,128)(2,1)}) %all-gather.5.cloned.1.call-update) | async-done | bytes 2621456 | tf_op jit(solution)/shard_map/all_gather | solution.py:83
  122.2 3.2 convolution_convert_fusion.4
  125.7 1.2 broadcast.209.clone
  128.5 14.6 %all-reduce.6.cloned.1.call-done = bf16[64,5120]{1,0:T(8,128)(2,1)} async-done(((bf16[64,5120]{1,0:T(8,128)(2,1)}), bf16[64,5120]{1,0:T(8,128)(2,1)}) %all-reduce.6.cloned.1.call-update) | async-done | bytes 655376 | tf_op jit(solution)/shard_map/psum | solution.py:117
  143.2 1.2 copy-done.14
  144.4 1.4 bitcast_dynamic-update-slice_fusion.5
  145.8 3.7 collective-permute-start
  150.7 13.2 %collective-permute-done = bf16[64,5120]{1,0:T(8,128)(2,1)S(1)} collective-permute-done((bf16[64,5120]{1,0:T(8,128)(2,1)S(1)}, bf16[64,5120]{1,0:T(8,128)(2,1)S(1)}, u32[]{:S(2)}, u32[]{:S(2)}) %collective-permute-start) | collective-permute-done | bytes 655392 | tf_op jit(solution)/shard_map/ppermute | solution.py:18
  167.0 1.5 convolution_convert_fusion.3
  168.6 2.0 constant_dynamic-slice_fusion.14
  170.6 2.0 constant_dynamic-slice_fusion.8
  172.6 16.8 %all-reduce.8.cloned.1.call-done = bf16[64,5120]{1,0:T(8,128)(2,1)} async-done(((bf16[64,5120]{1,0:T(8,128)(2,1)}), bf16[64,5120]{1,0:T(8,128)(2,1)}) %all-reduce.8.cloned.1.call-update) | async-done | bytes 655376 | tf_op jit(solution)/shard_map/psum | solution.py:117
  189.4 2.5 bitcast_dynamic-update-slice_fusion.4
  191.9 3.7 collective-permute-start.1
  195.6 2.2 constant_dynamic-slice_fusion.13
  197.8 12.1 %collective-permute-done.1 = bf16[64,5120]{1,0:T(8,128)(2,1)S(1)} collective-permute-done((bf16[64,5120]{1,0:T(8,128)(2,1)S(1)}, bf16[64,5120]{1,0:T(8,128)(2,1)S(1)}, u32[]{:S(2)}, u32[]{:S(2)}) %collective-permute-start.1) | collective-permute-done | bytes 655392 | tf_op jit(solution)/shard_map/ppermute | solution.py:18
  210.1 1.4 bitcast_dynamic-update-slice_fusion.2
  213.9 1.4 convolution_convert_fusion.2
  215.4 1.2 constant_dynamic-slice_fusion.17
  219.3 17.0 %all-reduce.10.cloned.1.call-done = bf16[64,5120]{1,0:T(8,128)(2,1)} async-done(((bf16[64,5120]{1,0:T(8,128)(2,1)}), bf16[64,5120]{1,0:T(8,128)(2,1)}) %all-reduce.10.cloned.1.call-update) | async-done | bytes 655376 | tf_op jit(solution)/shard_map/psum | solution.py:117
  236.2 3.1 bitcast_dynamic-update-slice_fusion.6
  239.3 2.4 fusion.32
  243.5 1.7 convolution_convert_fusion.1
  247.6 17.8 %all-reduce.12.cloned.1.call-done = bf16[64,5120]{1,0:T(8,128)(2,1)} async-done(((bf16[64,5120]{1,0:T(8,128)(2,1)}), bf16[64,5120]{1,0:T(8,128)(2,1)}) %all-reduce.12.cloned.1.call-update) | async-done | bytes 655376 | tf_op jit(solution)/shard_map/psum | solution.py:144
  265.4 2.1 fusion.48
  267.6 1.6 fusion.46
  269.2 1.5 collective-permute-start.2
  271.8 16.1 %collective-permute-done.2 = bf16[64,5120]{1,0:T(8,128)(2,1)S(1)} collective-permute-done((bf16[64,5120]{1,0:T(8,128)(2,1)S(1)}, bf16[64,5120]{1,0:T(8,128)(2,1)S(1)}, u32[]{:S(2)}, u32[]{:S(2)}) %collective-permute-start.2) | collective-permute-done | bytes 655392 | tf_op jit(solution)/shard_map/ppermute | solution.py:18
  288.0 1.2 bitcast_dynamic-update-slice_fusion.1
  291.7 1.7 convolution_convert_fusion
  293.5 19.2 %all-reduce.14.cloned.1.call-done = bf16[64,5120]{1,0:T(8,128)(2,1)} async-done(((bf16[64,5120]{1,0:T(8,128)(2,1)}), bf16[64,5120]{1,0:T(8,128)(2,1)}) %all-reduce.14.cloned.1.call-update) | async-done | bytes 655376 | tf_op jit(solution)/shard_map/psum | solution.py:144
  312.7 1.7 fusion.53
  314.4 1.7 fusion.52
  316.1 1.3 collective-permute-start.3
  318.6 16.3 %collective-permute-done.3 = bf16[64,5120]{1,0:T(8,128)(2,1)S(1)} collective-permute-done((bf16[64,5120]{1,0:T(8,128)(2,1)S(1)}, bf16[64,5120]{1,0:T(8,128)(2,1)S(1)}, u32[]{:S(2)}, u32[]{:S(2)}) %collective-permute-start.3) | collective-permute-done | bytes 655392 | tf_op jit(solution)/shard_map/ppermute | solution.py:18
  337.1 1.2 bitcast_dynamic-update-slice_fusion
  338.3 2.2 fusion.1
  340.5 2.7 pad_maximum_fusion
  344.5 12.9 %psum.47 = f32[]{:T(128)} all-reduce(f32[]{:T(128)} %convert_reduce_fusion), channel_id=1, replica_groups=mesh['groups'=2,'dp'=4,'section'=2,'tensor'=2] {'dp'}, use_global_device_ids=true, to_apply=%region_17.20 | all-reduce | flops 1 | bytes 8 | tf_op jit(solution)/shard_map/psum | solution.py:168
  357.4 80.2 %reduce-scatter.2.cloned.1.call-done = bf16[1280,512]{0,1:T(8,128)(2,1)} async-done(((bf16[5120,512]{0,1:T(8,128)(2,1)}), bf16[1280,512]{0,1:T(8,128)(2,1)}) %reduce-scatter.2.cloned.1.call-update) | async-done | bytes 1310736 | tf_op jit(solution)/shard_map/reduce_scatter | solution.py:156
  437.6 2.2 convert_divide_fusion
  439.7 1.2 slice_bitcast_fusion
  441.0 1.5 copy.18
  (126 shorter events, 28.8 us)
Async XLA Ops:
  7.2 2.3 copy-start
  7.2 1.6 copy-start.30
  7.2 1.6 copy-start.1
  7.2 59.9 %all-gather.3.cloned.1.call-start = ((), (), s32[]{:S(2)}) async-start(), calls=%async_computation.1 | async-start | bytes 3276800 | tf_op jit(solution)/shard_map/all_gather | solution.py:82
  7.9 114.3 %all-gather.5.cloned.1.call-start = ((), (), s32[]{:S(2)}) async-start(), calls=%async_computation.2 | async-start | bytes 3276800 | tf_op jit(solution)/shard_map/all_gather | solution.py:83
  8.7 134.4 %all-reduce.6.cloned.1.call-start = ((), (), s32[]{:S(2)}) async-start(), calls=%async_computation.3 | async-start | bytes 1310720 | tf_op jit(solution)/shard_map/psum | solution.py:117
  9.5 1.7 copy-start.27
  11.2 1.7 copy-start.2
  11.2 2.4 copy-start.28
  11.2 3.0 copy-start.29
  14.8 52.3 %copy-start.26 = (f32[1,5120]{1,0:T(1,128)S(1)}, f32[1,5120]{1,0:T(1,128)}, u32[]{:S(2)}) copy-start(f32[1,5120]{1,0:T(1,128)} %param.19) | copy-start | bytes 61444
  16.8 1.1 copy-start.12
  125.4 64.0 %all-reduce.8.cloned.1.call-start = ((), (), s32[]{:S(2)}) async-start(), calls=%async_computation.4 | async-start | bytes 1310720 | tf_op jit(solution)/shard_map/psum | solution.py:117
  125.7 1.8 copy-start.13
  143.1 1.3 copy-start.14
  145.8 4.9 %copy-start.20 = (bf16[2,64,5120]{2,1,0:T(8,128)(2,1)}, bf16[2,64,5120]{2,1,0:T(8,128)(2,1)S(1)}, u32[]{:S(2)}) copy-start(bf16[2,64,5120]{2,1,0:T(8,128)(2,1)S(1)} %get-tuple-element.22) | copy-start | bytes 3932164
  145.8 18.1 %collective-permute-start = (bf16[64,5120]{1,0:T(8,128)(2,1)S(1)}, bf16[64,5120]{1,0:T(8,128)(2,1)S(1)}, u32[]{:S(2)}, u32[]{:S(2)}) collective-permute-start(bf16[64,5120]{1,0:T(8,128)(2,1)S(1)} %get-tuple-element.23), channel_id=1, source_target_pairs={{0,2},{1,3},{4,6},{5,7},{8,10},{9,11},{12,14},{13,15},{16,18},{17,... | collective-permute-start | bytes 1966088 | tf_op jit(solution)/shard_map/ppermute | solution.py:18
  150.7 14.6 %copy-start.8 = (bf16[1,5120,256]{2,1,0:T(8,128)(2,1)S(1)}, bf16[1,5120,256]{2,1,0:T(8,128)(2,1)}, u32[]{:S(2)}) copy-start(bf16[1,5120,256]{2,1,0:T(8,128)(2,1)} %all-gather.3.cloned.1.call-done) | copy-start | bytes 7864324
  165.3 1.7 copy-start.3
  168.5 67.7 %all-reduce.10.cloned.1.call-start = ((), (), s32[]{:S(2)}) async-start(), calls=%async_computation.5 | async-start | bytes 1310720 | tf_op jit(solution)/shard_map/psum | solution.py:117
  191.9 18.1 %collective-permute-start.1 = (bf16[64,5120]{1,0:T(8,128)(2,1)S(1)}, bf16[64,5120]{1,0:T(8,128)(2,1)S(1)}, u32[]{:S(2)}, u32[]{:S(2)}) collective-permute-start(bf16[64,5120]{1,0:T(8,128)(2,1)S(1)} %get-tuple-element.21), channel_id=1, source_target_pairs={{0,2},{1,3},{4,6},{5,7},{8,10},{9,11},{12,14},{13,15},{16,18},{17,... | collective-permute-start | bytes 1966088 | tf_op jit(solution)/shard_map/ppermute | solution.py:18
  195.6 14.5 %copy-start.15 = (bf16[16,8,5120]{2,1,0:T(8,128)(2,1)S(1)}, bf16[16,8,5120]{2,1,0:T(8,128)(2,1)}, u32[]{:S(2)}) copy-start(bf16[16,8,5120]{2,1,0:T(8,128)(2,1)} %copy-done.12) | copy-start | bytes 3932164
  195.6 14.5 %copy-start.25 = (bf16[1,64,5120]{2,1,0:T(8,128)(2,1)S(1)}, bf16[1,64,5120]{2,1,0:T(8,128)(2,1)}, u32[]{:S(2)}) copy-start(bf16[1,64,5120]{2,1,0:T(8,128)(2,1)} %constant_dynamic-slice_fusion.8) | copy-start | bytes 1966084
  210.1 2.0 copy-start.9
  211.5 1.2 copy-start.16
  211.5 1.3 copy-start.21
  212.0 1.9 copy-start.4
  215.4 50.0 %all-reduce.12.cloned.1.call-start = ((), (), s32[]{:S(2)}) async-start(), calls=%async_computation.6 | async-start | bytes 1310720 | tf_op jit(solution)/shard_map/psum | solution.py:144
  215.4 1.5 copy-start.17
  217.3 1.1 copy-start.18
  218.4 17.8 %copy-start.22 = (bf16[64,5120]{1,0:T(8,128)(2,1)S(1)}, bf16[64,5120]{1,0:T(8,128)(2,1)}, u32[]{:S(2)}) copy-start(bf16[64,5120]{1,0:T(8,128)(2,1)} %copy-done.21) | copy-start | bytes 1966084
  239.3 2.4 copy-start.5
  241.8 1.7 copy-start.10
  245.3 67.4 %all-reduce.14.cloned.1.call-start = ((), (), s32[]{:S(2)}) async-start(), calls=%async_computation.7 | async-start | bytes 1310720 | tf_op jit(solution)/shard_map/psum | solution.py:144
  265.4 2.1 copy-start.24
  269.2 18.8 %collective-permute-start.2 = (bf16[64,5120]{1,0:T(8,128)(2,1)S(1)}, bf16[64,5120]{1,0:T(8,128)(2,1)S(1)}, u32[]{:S(2)}, u32[]{:S(2)}) collective-permute-start(bf16[64,5120]{1,0:T(8,128)(2,1)S(1)} %fusion.46), channel_id=1, source_target_pairs={{2,0},{3,1},{6,4},{7,5},{10,8},{11,9},{14,12},{15,13},{18,16},{19,... | collective-permute-start | bytes 1966088 | tf_op jit(solution)/shard_map/ppermute | solution.py:18
  288.0 2.0 copy-start.6
  290.0 1.7 copy-start.11
  293.5 144.1 %reduce-scatter.2.cloned.1.call-start = ((), (), s32[]{:S(2)}) async-start(), calls=%async_computation.8 | async-start | bytes 6553600 | tf_op jit(solution)/shard_map/reduce_scatter | solution.py:156
  312.7 1.7 copy-start.23
  314.4 20.5 %copy-start.7 = (bf16[1,256,5120]{2,1,0:T(8,128)(2,1)S(1)}, bf16[1,256,5120]{2,1,0:T(8,128)(2,1)}, u32[]{:S(2)}) copy-start(bf16[1,256,5120]{2,1,0:T(8,128)(2,1)} %all-gather.5.cloned.1.call-done) | copy-start | bytes 7864324
  316.1 18.8 %collective-permute-start.3 = (bf16[64,5120]{1,0:T(8,128)(2,1)S(1)}, bf16[64,5120]{1,0:T(8,128)(2,1)S(1)}, u32[]{:S(2)}, u32[]{:S(2)}) collective-permute-start(bf16[64,5120]{1,0:T(8,128)(2,1)S(1)} %fusion.52), channel_id=1, source_target_pairs={{2,0},{3,1},{6,4},{7,5},{10,8},{11,9},{14,12},{15,13},{18,16},{19,... | collective-permute-start | bytes 1966088 | tf_op jit(solution)/shard_map/ppermute | solution.py:18
  334.9 1.3 copy-start.19
Sparse Core Ops, SparseCore 0:
  9.6 57.4 all-gather.2
  68.6 53.4 all-gather.4
  125.5 17.5 all-reduce.5
  168.6 20.6 all-reduce.7
  215.5 20.6 all-reduce.9
  245.4 19.9 all-reduce.11
  293.6 19.0 all-reduce.13
  343.3 94.1 reduce-scatter.1
where the time goes:
time: 450 us; the launch traced here: 449 us
  waiting for transfers between devices  326 us (72%)
  local copies, waits for them, and re-layouts  32.9 us (7%)
  other arithmetic  32.2 us (7%)
  matrix products  19.3 us (4%)
  between operations  15.3 us (3%)
  blocking collectives  12.9 us (3%)
  starting transfers between devices  10.5 us (2%)
    reduce_scatter x1, waiting for transfers between devices, local(): lax.psum_scatter(jnp.concatenate([contract_first(flat_normed, flat_grad_v...  80.2 us
    ppermute x4, waiting for transfers between devices, from_behind(): return lax.ppermute(block, axis, route)  57.8 us
    all_gather x1, waiting for transfers between devices, local(): lax.all_gather(output_proj, 'dp', axis=2, tiled=True)  52.5 us
    all_gather x1, waiting for transfers between devices, local(): lax.all_gather(value_proj, 'dp', axis=1, tiled=True)  48.9 us
    psum x3, waiting for transfers between devices, local(): lax.psum(partial_out.astype(jnp.bfloat16), 'tensor').astype(jnp.float32)  48.4 us
    psum x2, waiting for transfers between devices, local(): lax.psum(partial_norm.astype(jnp.bfloat16), 'tensor').astype(jnp.float32)  37 us
    dynamic_update_slice x10, other arithmetic, put_slot(): lax.dynamic_update_index_in_dim(slot_store, jnp.where(active, new_value,...  14.3 us
    psum x1, blocking collectives, local(): token_total = lax.psum(local_count, 'dp')  12.9 us
  transfers between devices with their start and end apart: 12, of which 12 were waited for; matrix products, arithmetic and copies ran while one was open for 6% of the time, Pallas kernels for 0%

commit v1 on v0

--- a/solution.py
+++ b/solution.py
@@ -114,7 +114,9 @@
             jnp.bfloat16
         )
         partial_out = jnp.dot(projected, w_second, preferred_element_type=jnp.float32)
-        mixed_sum = lax.psum(partial_out.astype(jnp.bfloat16), "tensor").astype(jnp.float32)
+        mixed_sum = jnp.sum(
+            lax.all_gather(partial_out.astype(jnp.bfloat16), "tensor"), axis=0
+        ).astype(jnp.float32)
         leaving = (values + mixed_sum).astype(jnp.bfloat16)
         store_in = put_slot(store_in, entering, clamped, active)
         store_normed = put_slot(store_normed, normed, clamped, active)

time: 450 us -> 429 us (0.953)
  waiting for transfers between devices: 326 us -> 298 us
  other arithmetic: 32.2 us -> 39.4 us
    psum x3 -> x0, waiting for transfers between devices: 48.4 us -> none  [local(): lax.psum(partial_out.astype(jnp.bfloat16), 'tensor').astype(jnp.float32)]
    all_gather x0 -> x3, waiting for transfers between devices: none -> 18.3 us  [local(): lax.all_gather(partial_out.astype(jnp.bfloat16), 'tensor')]
    reduce_sum x0 -> x3, other arithmetic: none -> 6.78 us  [local(): jnp.sum(lax.all_gather(partial_out.astype(jnp.bfloat16), 'tensor'), axis=0)]
    dynamic_update_slice x10 -> x9, other arithmetic: 14.3 us -> 13.3 us  [put_slot(): lax.dynamic_update_index_in_dim(slot_store, jnp.where(active, new_value,...]
    unnamed x65 -> x69, local copies, waits for them, and re-layouts: 11.3 us -> 10.3 us
  transfers between devices with their start and end apart: 12 -> 12, of which waited for: 12 -> 12; matrix products, arithmetic and copies ran while one was open for 6% -> 7% of each run, Pallas kernels for 0% -> 0%
where the time goes in v1:
time: 429 us; the launch traced here: 428 us
  waiting for transfers between devices  298 us (69%)
  other arithmetic  39.4 us (9%)
  local copies, waits for them, and re-layouts  31.9 us (7%)
  matrix products  19.2 us (4%)
  between operations  15.4 us (4%)
  blocking collectives  12.9 us (3%)
  starting transfers between devices  10.6 us (2%)
    reduce_scatter x1, waiting for transfers between devices, local(): lax.psum_scatter(jnp.concatenate([contract_first(flat_normed, flat_grad_v...  80.1 us
    ppermute x4, waiting for transfers between devices, from_behind(): return lax.ppermute(block, axis, route)  58.1 us
    all_gather x1, waiting for transfers between devices, local(): lax.all_gather(output_proj, 'dp', axis=2, tiled=True)  52.5 us
    all_gather x1, waiting for transfers between devices, local(): lax.all_gather(value_proj, 'dp', axis=1, tiled=True)  50.9 us
    psum x2, waiting for transfers between devices, local(): lax.psum(partial_norm.astype(jnp.bfloat16), 'tensor').astype(jnp.float32)  36.8 us
    all_gather x3, waiting for transfers between devices, local(): lax.all_gather(partial_out.astype(jnp.bfloat16), 'tensor')  18.3 us
    dynamic_update_slice x9, other arithmetic, put_slot(): lax.dynamic_update_index_in_dim(slot_store, jnp.where(active, new_value,...  13.3 us
    psum x1, blocking collectives, local(): token_total = lax.psum(local_count, 'dp')  12.9 us
  transfers between devices with their start and end apart: 12, of which 12 were waited for; matrix products, arithmetic and copies ran while one was open for 7% of the time, Pallas kernels for 0%

profile of v1, /device:TPU:0, one launch (start us, length us, event | category | flops | bytes accessed | tf_op | source)
XLA Modules:
  0.0 427.6 jit_solution(14197899247860070260)
XLA Ops:
  9.5 1.7 gather_fusion.2
  11.2 1.7 gather_fusion.4
  12.9 2.0 broadcast_select_fusion.1
  16.2 50.9 %all-gather.9.cloned.1.call-done = bf16[1,5120,256]{2,1,0:T(8,128)(2,1)} async-done(((bf16[1,1280,256]{2,1,0:T(8,128)(2,1)}), bf16[1,5120,256]{2,1,0:T(8,128)(2,1)}) %all-gather.9.cloned.1.call-update) | async-done | bytes 2621456 | tf_op jit(solution)/shard_map/all_gather | solution.py:82
  67.1 2.6 bitcast_dynamic-update-slice_fusion.9
  69.7 52.5 %all-gather.11.cloned.1.call-done = bf16[1,256,5120]{2,1,0:T(8,128)(2,1)} async-done(((bf16[1,256,1280]{2,1,0:T(8,128)(2,1)}), bf16[1,256,5120]{2,1,0:T(8,128)(2,1)}) %all-gather.11.cloned.1.call-update) | async-done | bytes 2621456 | tf_op jit(solution)/shard_map/all_gather | solution.py:83
  122.2 3.2 convolution_convert_fusion.4
  130.2 3.5 all-gather.13.cloned.1.call-done
  133.7 1.6 reduce_sum.136
  135.4 1.6 fusion.31
  136.9 3.8 collective-permute-start
  141.9 13.2 %collective-permute-done = bf16[64,5120]{1,0:T(8,128)(2,1)S(1)} collective-permute-done((bf16[64,5120]{1,0:T(8,128)(2,1)S(1)}, bf16[64,5120]{1,0:T(8,128)(2,1)S(1)}, u32[]{:S(2)}, u32[]{:S(2)}) %collective-permute-start) | collective-permute-done | bytes 655392 | tf_op jit(solution)/shard_map/ppermute | solution.py:18
  155.3 1.4 bitcast_dynamic-update-slice_fusion.3
  159.0 1.4 convolution_convert_fusion.3
  160.7 2.0 constant_dynamic-slice_fusion.14
  162.8 2.0 constant_dynamic-slice_fusion.8
  164.8 7.1 %all-gather.15.cloned.1.call-done = bf16[128,5120]{1,0:T(8,128)(2,1)} async-done(((bf16[64,5120]{1,0:T(8,128)(2,1)}), bf16[128,5120]{1,0:T(8,128)(2,1)}) %all-gather.15.cloned.1.call-update) | async-done | bytes 1310736 | tf_op jit(solution)/shard_map/all_gather | solution.py:118
  171.9 2.6 reduce_sum.138
  174.5 2.5 bitcast_dynamic-update-slice_fusion.4
  177.0 3.7 collective-permute-start.1
  180.7 2.1 constant_dynamic-slice_fusion.13
  182.8 12.2 %collective-permute-done.1 = bf16[64,5120]{1,0:T(8,128)(2,1)S(1)} collective-permute-done((bf16[64,5120]{1,0:T(8,128)(2,1)S(1)}, bf16[64,5120]{1,0:T(8,128)(2,1)S(1)}, u32[]{:S(2)}, u32[]{:S(2)}) %collective-permute-start.1) | collective-permute-done | bytes 655392 | tf_op jit(solution)/shard_map/ppermute | solution.py:18
  195.2 1.4 bitcast_dynamic-update-slice_fusion.2
  199.0 1.4 convolution_convert_fusion.2
  200.6 1.2 constant_dynamic-slice_fusion.17
  204.4 7.6 %all-gather.17.cloned.1.call-done = bf16[128,5120]{1,0:T(8,128)(2,1)} async-done(((bf16[64,5120]{1,0:T(8,128)(2,1)}), bf16[128,5120]{1,0:T(8,128)(2,1)}) %all-gather.17.cloned.1.call-update) | async-done | bytes 1310736 | tf_op jit(solution)/shard_map/all_gather | solution.py:118
  212.0 2.6 reduce_sum.140
  214.6 3.1 bitcast_dynamic-update-slice_fusion.5
  217.7 2.4 fusion.28
  221.8 1.8 convolution_convert_fusion.1
  226.1 17.6 %all-reduce.3.cloned.1.call-done = bf16[64,5120]{1,0:T(8,128)(2,1)} async-done(((bf16[64,5120]{1,0:T(8,128)(2,1)}), bf16[64,5120]{1,0:T(8,128)(2,1)}) %all-reduce.3.cloned.1.call-update) | async-done | bytes 655376 | tf_op jit(solution)/shard_map/psum | solution.py:146
  243.8 2.1 fusion.49
  245.9 1.6 fusion.47
  247.5 1.3 collective-permute-start.2
  250.0 16.3 %collective-permute-done.2 = bf16[64,5120]{1,0:T(8,128)(2,1)S(1)} collective-permute-done((bf16[64,5120]{1,0:T(8,128)(2,1)S(1)}, bf16[64,5120]{1,0:T(8,128)(2,1)S(1)}, u32[]{:S(2)}, u32[]{:S(2)}) %collective-permute-start.2) | collective-permute-done | bytes 655392 | tf_op jit(solution)/shard_map/ppermute | solution.py:18
  270.0 1.7 convolution_convert_fusion
  271.9 19.2 %all-reduce.5.cloned.1.call-done = bf16[64,5120]{1,0:T(8,128)(2,1)} async-done(((bf16[64,5120]{1,0:T(8,128)(2,1)}), bf16[64,5120]{1,0:T(8,128)(2,1)}) %all-reduce.5.cloned.1.call-update) | async-done | bytes 655376 | tf_op jit(solution)/shard_map/psum | solution.py:146
  291.0 1.7 fusion.54
  292.7 1.7 fusion.53
  294.5 1.3 collective-permute-start.3
  296.9 16.3 %collective-permute-done.3 = bf16[64,5120]{1,0:T(8,128)(2,1)S(1)} collective-permute-done((bf16[64,5120]{1,0:T(8,128)(2,1)S(1)}, bf16[64,5120]{1,0:T(8,128)(2,1)S(1)}, u32[]{:S(2)}, u32[]{:S(2)}) %collective-permute-start.3) | collective-permute-done | bytes 655392 | tf_op jit(solution)/shard_map/ppermute | solution.py:18
  316.6 2.2 fusion.1
  318.8 2.7 pad_maximum_fusion
  322.8 12.9 %psum.23 = f32[]{:T(128)} all-reduce(f32[]{:T(128)} %convert_reduce_fusion), channel_id=1, replica_groups=mesh['groups'=2,'dp'=4,'section'=2,'tensor'=2] {'dp'}, use_global_device_ids=true, to_apply=%region_17.20 | all-reduce | flops 1 | bytes 8 | tf_op jit(solution)/shard_map/psum | solution.py:170
  335.7 80.1 %reduce-scatter.2.cloned.1.call-done = bf16[1280,512]{0,1:T(8,128)(2,1)} async-done(((bf16[5120,512]{0,1:T(8,128)(2,1)}), bf16[1280,512]{0,1:T(8,128)(2,1)}) %reduce-scatter.2.cloned.1.call-update) | async-done | bytes 1310736 | tf_op jit(solution)/shard_map/reduce_scatter | solution.py:158
  415.9 2.2 convert_divide_fusion
  418.0 1.2 slice_bitcast_fusion
  419.3 1.5 copy.18
  (133 shorter events, 31.7 us)
Async XLA Ops:
  7.2 2.3 copy-start
  7.2 1.6 copy-start.32
  7.2 1.6 copy-start.1
  7.2 59.9 %all-gather.9.cloned.1.call-start = ((), (), s32[]{:S(2)}) async-start(), calls=%async_computation.1 | async-start | bytes 3276800 | tf_op jit(solution)/shard_map/all_gather | solution.py:82
  7.9 114.3 %all-gather.11.cloned.1.call-start = ((), (), s32[]{:S(2)}) async-start(), calls=%async_computation.2 | async-start | bytes 3276800 | tf_op jit(solution)/shard_map/all_gather | solution.py:83
  8.7 125.0 %all-gather.13.cloned.1.call-start = ((), (), s32[]{:S(2)}) async-start(), calls=%async_computation.6 | async-start | bytes 1966080 | tf_op jit(solution)/shard_map/all_gather | solution.py:118
  9.5 1.7 copy-start.29
  12.8 54.2 %copy-start.28 = (f32[1,5120]{1,0:T(1,128)S(1)}, f32[1,5120]{1,0:T(1,128)}, u32[]{:S(2)}) copy-start(f32[1,5120]{1,0:T(1,128)} %param.19) | copy-start | bytes 61444
  14.8 1.1 copy-start.12
  122.2 3.3 copy-start.2
  122.2 3.9 copy-start.30
  125.4 1.4 copy-start.31
  125.4 46.5 %all-gather.15.cloned.1.call-start = ((), (), s32[]{:S(2)}) async-start(), calls=%async_computation.7 | async-start | bytes 1966080 | tf_op jit(solution)/shard_map/all_gather | solution.py:118
  127.4 1.8 copy-start.13
  135.3 6.5 %copy-start.23 = (bf16[64,5120]{1,0:T(8,128)(2,1)}, bf16[64,5120]{1,0:T(8,128)(2,1)S(1)}, u32[]{:S(2)}) copy-start(bf16[64,5120]{1,0:T(8,128)(2,1)S(1)} %reduce_sum.136) | copy-start | bytes 1966084
  136.9 18.4 %copy-start.14 = (bf16[16,8,5120]{2,1,0:T(8,128)(2,1)S(1)}, bf16[16,8,5120]{2,1,0:T(8,128)(2,1)}, u32[]{:S(2)}) copy-start(bf16[16,8,5120]{2,1,0:T(8,128)(2,1)} %copy-done.12) | copy-start | bytes 3932164
  136.9 18.2 %collective-permute-start = (bf16[64,5120]{1,0:T(8,128)(2,1)S(1)}, bf16[64,5120]{1,0:T(8,128)(2,1)S(1)}, u32[]{:S(2)}, u32[]{:S(2)}) collective-permute-start(bf16[64,5120]{1,0:T(8,128)(2,1)S(1)} %fusion.31), channel_id=1, source_target_pairs={{0,2},{1,3},{4,6},{5,7},{8,10},{9,11},{12,14},{13,15},{16,18},{17,... | collective-permute-start | bytes 1966088 | tf_op jit(solution)/shard_map/ppermute | solution.py:18
  141.9 13.4 %copy-start.24 = (bf16[64,5120]{1,0:T(8,128)(2,1)S(1)}, bf16[64,5120]{1,0:T(8,128)(2,1)}, u32[]{:S(2)}) copy-start(bf16[64,5120]{1,0:T(8,128)(2,1)} %copy-done.23) | copy-start | bytes 1966084
  155.3 2.0 copy-start.8
  156.7 1.2 copy-start.20
  157.3 1.7 copy-start.3
  160.4 51.6 %all-gather.17.cloned.1.call-start = ((), (), s32[]{:S(2)}) async-start(), calls=%async_computation.8 | async-start | bytes 1966080 | tf_op jit(solution)/shard_map/all_gather | solution.py:118
  177.0 18.1 %collective-permute-start.1 = (bf16[64,5120]{1,0:T(8,128)(2,1)S(1)}, bf16[64,5120]{1,0:T(8,128)(2,1)S(1)}, u32[]{:S(2)}, u32[]{:S(2)}) collective-permute-start(bf16[64,5120]{1,0:T(8,128)(2,1)S(1)} %get-tuple-element.21), channel_id=1, source_target_pairs={{0,2},{1,3},{4,6},{5,7},{8,10},{9,11},{12,14},{13,15},{16,18},{17,... | collective-permute-start | bytes 1966088 | tf_op jit(solution)/shard_map/ppermute | solution.py:18
  180.7 14.5 %copy-start.15 = (bf16[16,8,5120]{2,1,0:T(8,128)(2,1)S(1)}, bf16[16,8,5120]{2,1,0:T(8,128)(2,1)}, u32[]{:S(2)}) copy-start(bf16[16,8,5120]{2,1,0:T(8,128)(2,1)} %copy-done.12) | copy-start | bytes 3932164
  180.7 14.5 %copy-start.27 = (bf16[1,64,5120]{2,1,0:T(8,128)(2,1)S(1)}, bf16[1,64,5120]{2,1,0:T(8,128)(2,1)}, u32[]{:S(2)}) copy-start(bf16[1,64,5120]{2,1,0:T(8,128)(2,1)} %constant_dynamic-slice_fusion.8) | copy-start | bytes 1966084
  195.2 2.0 copy-start.9
  196.6 1.2 copy-start.16
  196.6 1.3 copy-start.21
  197.2 1.9 copy-start.4
  200.5 43.3 %all-reduce.3.cloned.1.call-start = ((), (), s32[]{:S(2)}) async-start(), calls=%async_computation.3 | async-start | bytes 1310720 | tf_op jit(solution)/shard_map/psum | solution.py:146
  200.5 1.5 copy-start.17
  202.4 1.1 copy-start.18
  204.4 10.2 %copy-start.22 = (bf16[64,5120]{1,0:T(8,128)(2,1)S(1)}, bf16[64,5120]{1,0:T(8,128)(2,1)}, u32[]{:S(2)}) copy-start(bf16[64,5120]{1,0:T(8,128)(2,1)} %copy-done.21) | copy-start | bytes 1966084
  217.7 2.4 copy-start.5
  220.1 1.7 copy-start.10
  223.6 67.4 %all-reduce.5.cloned.1.call-start = ((), (), s32[]{:S(2)}) async-start(), calls=%async_computation.4 | async-start | bytes 1310720 | tf_op jit(solution)/shard_map/psum | solution.py:146
  243.7 2.1 copy-start.26
  247.5 18.8 %collective-permute-start.2 = (bf16[64,5120]{1,0:T(8,128)(2,1)S(1)}, bf16[64,5120]{1,0:T(8,128)(2,1)S(1)}, u32[]{:S(2)}, u32[]{:S(2)}) collective-permute-start(bf16[64,5120]{1,0:T(8,128)(2,1)S(1)} %fusion.47), channel_id=1, source_target_pairs={{2,0},{3,1},{6,4},{7,5},{10,8},{11,9},{14,12},{15,13},{18,16},{19,... | collective-permute-start | bytes 1966088 | tf_op jit(solution)/shard_map/ppermute | solution.py:18
  266.3 2.0 copy-start.6
  268.3 1.7 copy-start.11
  271.8 144.1 %reduce-scatter.2.cloned.1.call-start = ((), (), s32[]{:S(2)}) async-start(), calls=%async_computation.5 | async-start | bytes 6553600 | tf_op jit(solution)/shard_map/reduce_scatter | solution.py:158
  291.0 1.7 copy-start.25
  292.7 20.5 %copy-start.7 = (bf16[1,256,5120]{2,1,0:T(8,128)(2,1)S(1)}, bf16[1,256,5120]{2,1,0:T(8,128)(2,1)}, u32[]{:S(2)}) copy-start(bf16[1,256,5120]{2,1,0:T(8,128)(2,1)} %all-gather.11.cloned.1.call-done) | copy-start | bytes 7864324
  294.5 18.8 %collective-permute-start.3 = (bf16[64,5120]{1,0:T(8,128)(2,1)S(1)}, bf16[64,5120]{1,0:T(8,128)(2,1)S(1)}, u32[]{:S(2)}, u32[]{:S(2)}) collective-permute-start(bf16[64,5120]{1,0:T(8,128)(2,1)S(1)} %fusion.53), channel_id=1, source_target_pairs={{2,0},{3,1},{6,4},{7,5},{10,8},{11,9},{14,12},{15,13},{18,16},{19,... | collective-permute-start | bytes 1966088 | tf_op jit(solution)/shard_map/ppermute | solution.py:18
  313.2 1.3 copy-start.19
Sparse Core Ops, SparseCore 0:
  9.6 57.4 all-gather.8
  68.6 53.5 all-gather.10
  125.5 8.1 all-gather.12
  160.6 11.3 all-gather.14
  200.6 11.3 all-gather.16
  223.8 19.9 all-reduce.2
  271.9 19.0 all-reduce.4
  321.7 94.1 reduce-scatter.1
